TPU v7x, 128 devices: a whole 4x4x4 slice. The times are simulated.
128 devices in a mesh: rep: 16 (over x_lo, y, core), tp: 8 (over z, x_hi).
Axes of the slice: x: 4 (x_hi: 2, x_lo: 2; x = x_hi * 2 + x_lo), y: 4, z: 4, core: 2. Of those that a mesh axis runs over, the one named last changes fastest.
Arguments:
- tokens: bfloat16 [16384, 1280], P(('rep', 'tp')), may hold values from -6 to 6
- view_ids: int32 [64, 4], P('rep'), may hold values from 0 to 31
- time_ids: int32 [64], P('rep'), may hold values from 0 to 999
- camera_table: float32 [32, 1280], replicated, may hold values from -6 to 6
- norm_attn: float32 [2, 1280], replicated, may hold values from 0.1 to 1.9
- norm_ffn: float32 [2, 1280], replicated, may hold values from 0.1 to 1.9
- w_query: bfloat16 [2, 1280, 1280], P(None, ('rep', 'tp')), may hold values from -0.1677051 to 0.1677051
- w_key: bfloat16 [2, 1280, 1280], P(None, ('rep', 'tp')), may hold values from -6.764106 to 6.764106
- w_value: bfloat16 [2, 1280, 1280], P(None, ('rep', 'tp')), may hold values from -0.15625 to 0.15625
- w_out: bfloat16 [2, 1280, 1280], P(None, ('rep', 'tp')), may hold values from -0.15625 to 0.15625
- w_gate: bfloat16 [2, 1280, 5120], P(None, ('rep', 'tp')), may hold values from -0.15625 to 0.15625
- w_up: bfloat16 [2, 1280, 5120], P(None, ('rep', 'tp')), may hold values from -0.15625 to 0.15625
- w_down: bfloat16 [2, 1280, 5120], P(None, ('rep', 'tp')), may hold values from -0.078125 to 0.078125
Outputs:
- denoised: bfloat16 [16384, 1280], P(('rep', 'tp'))
All inputs are finite; a program needn't handle non-finite values.
Results may differ from a plain program's by a relative error of at most 0.035.
Values may be sent and summed in bfloat16 or wider, within the bound.
A program may use at most 128 MiB of HBM per device.

v0:
```python
import math

import jax
import jax.numpy as jnp
from jax import lax
from jax.sharding import PartitionSpec as P

D = 1280
HEADS = 8
VIEWS = 4
HW = 64
LAYERS = 2


def sent_together(arrays, axis, split_dim, concat_dim, along):
    both = jnp.concatenate(arrays, axis=along)
    out, at, finished = (
        lax.all_to_all(both, axis, split_axis=split_dim, concat_axis=concat_dim, tiled=True),
        0,
        [],
    )
    for a in arrays:
        finished.append(lax.slice_in_dim(out, at, at + a.shape[along], axis=along))
        at += a.shape[along]
    return tuple(finished)


def side_by_side(arrays, axis, dim, along):
    ends, at = ([], 0)
    for a in arrays[:-1]:
        at += a.shape[along]
        ends.append(at)
    both = jnp.concatenate(arrays, axis=along)
    return tuple(jnp.split(lax.all_gather(both, axis, axis=dim, tiled=True), ends, axis=along))


def copy_for_each(shard, axis):
    size = lax.axis_size(axis)
    return lax.all_to_all(
        jnp.broadcast_to(shard[None], (size, *shard.shape)), axis, 0, 0, tiled=True
    )


def joined_along(blocks, dim):
    blocks = jnp.moveaxis(blocks, 0, dim)
    shape = blocks.shape
    return blocks.reshape(*shape[:dim], shape[dim] * shape[dim + 1], *shape[dim + 2 :])


def gathered_copies(shard, axis, dim):
    blocks = copy_for_each(shard, axis)
    return joined_along(blocks, dim)


def in_blocks(shard, dim, size):
    before, after = (shard.shape[:dim], shard.shape[dim + 1 :])
    return jnp.moveaxis(shard.reshape(*before, size, -1, *after), dim, 0)


def sum_at_owner(shard, axis, dim):
    blocks = in_blocks(shard, dim, lax.axis_size(axis))
    arrived = lax.all_to_all(blocks, axis, split_axis=0, concat_axis=0, tiled=True)
    return arrived.astype(jnp.float32).sum(axis=0)


def layer_norm(activations, gain_vector):
    average = jnp.mean(activations, axis=-1, keepdims=True)
    centred = activations - average
    spread = jnp.mean(centred * centred, axis=-1, keepdims=True)
    return (centred * lax.rsqrt(spread + 1e-05) * gain_vector).astype(jnp.bfloat16)


def time_code(step_ids, width):
    half_width = width // 2
    frequency = jnp.exp(-math.log(10000.0) * jnp.arange(half_width, dtype=jnp.float32) / half_width)
    angles = step_ids.astype(jnp.float32)[:, None] * frequency[None, :]
    return jnp.concatenate([jnp.cos(angles), jnp.sin(angles)], axis=1)


def conditioning(row_ids, view_ids, time_ids, camera_table):
    set_ids = row_ids // (VIEWS * HW)
    slot_ids = set_ids * VIEWS + row_ids // HW % VIEWS
    flat_views = view_ids.reshape(-1)
    slot_range = jnp.arange(flat_views.shape[0], dtype=jnp.int32)
    pose_ids = jnp.sum(
        jnp.where(slot_ids[:, None] == slot_range[None, :], flat_views[None, :], 0), axis=1
    )
    set_range = jnp.arange(time_ids.shape[0], dtype=jnp.int32)
    step_ids = jnp.sum(
        jnp.where(set_ids[:, None] == set_range[None, :], time_ids[None, :], 0), axis=1
    )
    pose_range = jnp.arange(camera_table.shape[0], dtype=jnp.int32)
    onehot_pose = (pose_ids[:, None] == pose_range[None, :]).astype(jnp.float32)
    camera = jnp.dot(onehot_pose, camera_table)
    return camera + time_code(step_ids, camera_table.shape[1])


def reshard(weights):
    owned = (
        *sent_together((weights[0], weights[1], weights[2], weights[3]), "tp", 2, 1, 0),
        *sent_together((weights[4], weights[5], weights[6]), "tp", 2, 1, 0),
    )
    return side_by_side(
        (owned[0], owned[1], owned[2], owned[3], owned[4], owned[5], owned[6]), "rep", 1, 2
    )


def attend(packed, width_local, head_size):
    total_rows = packed.shape[0]
    set_count = total_rows // (VIEWS * HW)
    heads_here = width_local // head_size
    shape_heads = (set_count, VIEWS * HW, heads_here, head_size)
    query_rows = packed[:, :width_local].reshape(shape_heads)
    key_rows = packed[:, width_local : 2 * width_local].reshape(shape_heads)
    value_rows = packed[:, 2 * width_local :].reshape(shape_heads)
    scores = jnp.einsum(
        "bqhd,bkhd->bhqk", query_rows, key_rows, preferred_element_type=jnp.float32
    ) * head_size ** (-0.5)
    peak = jnp.max(scores, axis=-1, keepdims=True)
    expons = jnp.exp(scores - peak)
    attn_probs = (expons / jnp.sum(expons, axis=-1, keepdims=True)).astype(jnp.bfloat16)
    mixed_rows = jnp.einsum(
        "bhqk,bkhd->bqhd", attn_probs, value_rows, preferred_element_type=jnp.float32
    )
    return mixed_rows.astype(jnp.bfloat16).reshape(total_rows, width_local)


def out_terms(mixed_rows, weight):
    return lax.dot_general(
        mixed_rows, weight, (((1,), (1,)), ((), ())), preferred_element_type=jnp.float32
    )


def body(
    tokens,
    view_ids,
    time_ids,
    camera_table,
    norm_attn,
    norm_ffn,
    w_query,
    w_key,
    w_value,
    w_out,
    w_gate,
    w_up,
    w_down,
):
    query_w, key_w, value_w, out_w, gate_w, up_w, down_w = reshard(
        (w_query, w_key, w_value, w_out, w_gate, w_up, w_down)
    )
    width_local = query_w.shape[2]
    head_size = D // HEADS
    share_rows = tokens.shape[0]
    first_row = lax.axis_index("tp") * share_rows
    row_ids = first_row + jnp.arange(share_rows, dtype=jnp.int32)
    stream = tokens.astype(jnp.float32) + conditioning(row_ids, view_ids, time_ids, camera_table)

    def spread_rows(normed, project):
        return project(gathered_copies(normed, "tp", 0), jnp.int32(0))

    def reduce_rows(mixed_rows, weight):
        return sum_at_owner(out_terms(mixed_rows, weight).astype(jnp.bfloat16), "tp", 0)

    for layer_index in range(LAYERS):
        query_here = query_w[layer_index]
        key_here = key_w[layer_index]
        value_here = value_w[layer_index]
        gate_here = gate_w[layer_index]
        up_here = up_w[layer_index]

        def project_attn(piece_rows, row_start):
            return jnp.concatenate(
                [
                    jnp.dot(piece_rows, query_here, preferred_element_type=jnp.float32).astype(
                        jnp.bfloat16
                    ),
                    jnp.dot(piece_rows, key_here, preferred_element_type=jnp.float32).astype(
                        jnp.bfloat16
                    ),
                    jnp.dot(piece_rows, value_here, preferred_element_type=jnp.float32).astype(
                        jnp.bfloat16
                    ),
                ],
                axis=1,
            )

        def project_ffn(piece_rows, row_start):
            gate_part = jnp.dot(piece_rows, gate_here, preferred_element_type=jnp.float32)
            up_part = jnp.dot(piece_rows, up_here, preferred_element_type=jnp.float32)
            return (jax.nn.gelu(gate_part, approximate=False) * up_part).astype(jnp.bfloat16)

        normed = layer_norm(stream, norm_attn[layer_index])
        packed = spread_rows(normed, project_attn)
        mixed_rows = attend(packed, width_local, head_size)
        stream = stream + reduce_rows(mixed_rows, out_w[layer_index])
        normed = layer_norm(stream, norm_ffn[layer_index])
        hidden = spread_rows(normed, project_ffn)
        stream = stream + reduce_rows(hidden, down_w[layer_index])
    return stream.astype(jnp.bfloat16)


def solution(mesh):
    return jax.shard_map(
        body,
        mesh=mesh,
        in_specs=(
            P(("rep", "tp"), None),
            P("rep", None),
            P("rep"),
            P(),
            P(),
            P(),
            P(None, ("rep", "tp"), None),
            P(None, ("rep", "tp"), None),
            P(None, ("rep", "tp"), None),
            P(None, ("rep", "tp"), None),
            P(None, ("rep", "tp"), None),
            P(None, ("rep", "tp"), None),
            P(None, ("rep", "tp"), None),
        ),
        out_specs=P(("rep", "tp"), None),
        check_vma=False,
    )
```

profile of v0, /device:TPU:1, one launch (start us, length us, event | category | flops | bytes accessed | tf_op | source)
XLA Modules:
  0.0 562.5 jit_solution(8468619610779781675)
XLA Ops:
  6.5 1.2 pad_maximum_fusion.1
  7.7 1.9 copy.115
  9.7 5.5 reshape.234
  15.2 8.3 %all-to-all-start.1 = ((bf16[8,2,6400]{2,1,0:T(2,128)(2,1)}), bf16[8,2,6400]{2,1,0:T(2,128)(2,1)S(1)}, u32[]{:S(2)}, u32[]{:S(2)}) async-start(bf16[8,2,6400]{2,1,0:T(2,128)(2,1)} %reshape.234), calls=%async_computation.1 | async-start | bytes 409600 | tf_op jit(solution)/shard_map/all_to_all | solution.py:18
  23.5 0.7 pad_maximum_fusion
  24.2 8.6 %copy.117 = bf16[6,10,5120]{1,0,2:T(8,128)(2,1)} copy(bf16[6,10,5120]{2,0,1:T(8,128)(2,1)S(1)} %pad_maximum_fusion) | data formatting | bytes 1228800 | tf_op jit(solution)/shard_map/concatenate | solution.py:16
  32.8 12.3 %reshape.236 = bf16[8,2,19200]{2,1,0:T(2,128)(2,1)} reshape(bf16[5120,6,10]{2,1,0:T(8,128)(2,1)} %bitcast.148) | data formatting | bytes 1228800
  45.0 6.6 %all-to-all-start.2 = ((bf16[8,2,19200]{2,1,0:T(2,128)(2,1)}), bf16[8,2,19200]{2,1,0:T(2,128)(2,1)S(1)}, u32[]{:S(2)}, u32[]{:S(2)}) async-start(bf16[8,2,19200]{2,1,0:T(2,128)(2,1)} %reshape.236), calls=%async_computation.2 | async-start | bytes 1228800 | tf_op jit(solution)/shard_map/all_to_all | solution.py:18
  51.9 6.9 %reshape.235 = bf16[1280,8,10]{2,1,0:T(8,128)(2,1)S(1)} reshape(bf16[8,2,6400]{2,1,0:T(2,128)(2,1)} %copy-done.8) | data formatting | bytes 409600
  58.8 2.4 copy.116
  61.3 1.8 fusion.143
  63.1 11.8 %reshape.237 = bf16[5120,6,10]{2,1,0:T(8,128)(2,1)} reshape(bf16[8,2,19200]{2,1,0:T(2,128)(2,1)S(1)} %all-to-all-done.2) | data formatting | bytes 1228800
  74.9 10.2 %copy.118 = bf16[6,10,8,640]{3,0,1,2:T(8,128)(2,1)S(1)} copy(bf16[6,10,8,640]{1,0,3,2:T(8,128)(2,1)} %bitcast.149) | data formatting | bytes 1228800 | tf_op jit(solution)/shard_map/all_to_all | solution.py:18
  85.1 0.4 fusion.142
  85.6 3.9 concatenate.15
  89.9 1.2 multiply_cosine_fusion
  91.1 0.4 fusion.144
  91.9 1.6 broadcast_in_dim.39
  93.6 6.9 %all-to-all-start = ((bf16[8,128,1280]{2,1,0:T(8,128)(2,1)}), bf16[8,128,1280]{2,1,0:T(8,128)(2,1)}, u32[]{:S(2)}, u32[]{:S(2)}) async-start(bf16[8,128,1280]{2,1,0:T(8,128)(2,1)} %broadcast_in_dim.39), calls=%async_computation | async-start | bytes 5242880 | tf_op jit(solution)/shard_map/all_to_all | solution.py:39
  100.5 93.0 %all-gather.2.cloned.1.call-done = bf16[2,1280,2560]{2,0,1:T(2,128)(2,1)} async-done(((bf16[2,80,2560]{2,0,1:T(2,128)(2,1)}), bf16[2,1280,2560]{2,0,1:T(2,128)(2,1)}) %all-gather.2.cloned.1.call-update) | async-done | bytes 13107216 | tf_op jit(solution)/shard_map/all_gather | solution.py:34
  193.5 20.0 %fusion.141 = (bf16[1,1280,160]{2,0,1:T(2,128)(2,1)}, bf16[1,1280,160]{2,0,1:T(2,128)(2,1)}, bf16[1,1280,160]{2,0,1:T(2,128)(2,1)}, bf16[1,1280,160]{2,0,1:T(2,1...) fusion(bf16[2,1280,2560]{2,0,1:T(2,128)(2,1)} %all-gather.2.clo, ...), kind=kLoop, calls=%fused_computation.212 | loop fusion | bytes 6553600 | tf_op jit(solution)/shard_map/slice | solution.py:196
  213.4 3.6 copy.148
  217.0 3.6 copy.147
  220.6 2.5 copy.146
  223.1 2.8 convolution_convert_fusion.9
  226.0 2.7 convolution_convert_fusion.10
  228.7 1.8 copy.145
  230.5 2.7 convolution_convert_fusion.11
  233.2 0.5 fusion.145
  233.8 0.3 fusion.31
  234.4 0.4 copy-done.7
  234.8 2.4 convolution_convert_fusion.3
  237.2 7.4 %all-to-all-start.3 = ((bf16[8,128,1280]{2,1,0:T(8,128)(2,1)}), bf16[8,128,1280]{2,1,0:T(8,128)(2,1)S(1)}, u32[]{:S(2)}, u32[]{:S(2)}) async-start(bf16[8,128,1280]{2,1,0:T(8,128)(2,1)} %bitcast.150), calls=%async_computation.3 | async-start | bytes 5242880 | tf_op jit(solution)/shard_map/all_to_all | solution.py:62
  244.6 33.6 %all-to-all-done.3 = bf16[8,128,1280]{2,1,0:T(8,128)(2,1)S(1)} async-done(((bf16[8,128,1280]{2,1,0:T(8,128)(2,1)}), bf16[8,128,1280]{2,1,0:T(8,128)(2,1)S(1)}, u32[]{:S(2)}, u32[]{:S(2)}) %all-to-all-start.3) | async-done | bytes 2621472 | tf_op jit(solution)/shard_map/all_to_all | solution.py:62
  278.2 0.3 convert_reduce_fusion.3
  279.1 1.7 broadcast_in_dim.40
  280.8 4.9 all-to-all-start.4
  285.7 21.6 %fusion.140 = (bf16[1,1280,640]{2,0,1:T(2,128)(2,1)}, bf16[1,1280,640]{2,0,1:T(2,128)(2,1)}, bf16[1,1280,640]{2,0,1:T(2,128)(2,1)}, bf16[1,1280,640]{2,0,1:T(2,1...) fusion(bf16[2,1280,2560]{2,0,1:T(2,128)(2,1)} %all-gather.2.cloned.1.call-done), kind=kLoop, calls=%fused_computation.211 | loop fusion | bytes 19660800 | tf_op jit(solution)/shard_map/slice | solution.py:170
  307.3 11.1 %all-to-all-done.4 = bf16[8,128,1280]{2,1,0:T(8,128)(2,1)} async-done(((bf16[8,128,1280]{2,1,0:T(8,128)(2,1)}), bf16[8,128,1280]{2,1,0:T(8,128)(2,1)}, u32[]{:S(2)}, u32[]{:S(2)}) %all-to-all-start.4) | async-done | bytes 2621472 | tf_op jit(solution)/shard_map/all_to_all | solution.py:39
  318.4 6.4 %fusion.26 = f32[1024,640]{1,0:T(8,128)} fusion(bf16[1024,1280]{1,0:T(8,128)(2,1)} %bitcast.19, bf16[1,1280,640]{2,0,1:T(2,128)(2,1)} %get-tuple-element.19), kind=kOutput, calls=%fused_computation.59 | convolution fusion | flops 1677721600 | bytes 6881280 | tf_op jit(solution)/shard_map/dot_general | solution.py:189
  324.8 14.4 %convolution_convert_fusion.1 = bf16[1024,1280]{1,0:T(8,128)(2,1)} fusion(bf16[1,1280,640]{2,0,1:T(2,128)(2,1)} %get-tuple-element.17, f32[1024,640]{1,0:T(8,128)} %fusion.26, bf16[1024,1280]{1,0:T(8,128)(2,1)} %bitcast.19, bf16[1,1280,640]{2,0,1:T(2,128)(2,1)} %get-tuple-element.18), kind=kOutput, calls=%fused_computation.9 | convolution fusion | flops 3400007680 | bytes 11141120 | tf_op jit(solution)/shard_map/dot_general | solution.py:129
  339.2 36.7 %all_to_all.70 = bf16[8,128,1280]{2,1,0:T(8,128)(2,1)S(1)} all-to-all(bf16[8,128,1280]{2,1,0:T(8,128)(2,1)} %bitcast.156), channel_id=1, replica_groups=mesh['rep'=16,'tp'=8] {'tp'}, dimensions={0} | all-to-all | bytes 5242880 | tf_op jit(solution)/shard_map/all_to_all | solution.py:62
  376.0 0.4 convert_reduce_fusion.2
  376.9 1.7 broadcast_in_dim.41
  378.6 4.6 all-to-all-start.6
  383.2 3.8 copy.155
  387.0 3.6 copy.154
  390.6 2.5 copy.153
  393.1 1.8 copy.152
  394.9 19.9 %all-to-all-done.6 = bf16[8,128,1280]{2,1,0:T(8,128)(2,1)} async-done(((bf16[8,128,1280]{2,1,0:T(8,128)(2,1)}), bf16[8,128,1280]{2,1,0:T(8,128)(2,1)}, u32[]{:S(2)}, u32[]{:S(2)}) %all-to-all-start.6) | async-done | bytes 2621472 | tf_op jit(solution)/shard_map/all_to_all | solution.py:39
  414.8 2.8 convolution_convert_fusion.5
  417.7 2.7 convolution_convert_fusion.6
  420.4 2.7 convolution_convert_fusion.7
  423.2 0.5 fusion.150
  424.3 0.4 copy-done.6
  424.7 0.9 convolution_convert_fusion.2
  425.6 38.2 %all_to_all.71 = bf16[8,128,1280]{2,1,0:T(8,128)(2,1)S(1)} all-to-all(bf16[8,128,1280]{2,1,0:T(8,128)(2,1)S(1)} %bitcast.151), channel_id=1, replica_groups=mesh['rep'=16,'tp'=8] {'tp'}, dimensions={0} | all-to-all | bytes 5242880 | tf_op jit(solution)/shard_map/all_to_all | solution.py:62
  463.8 0.4 convert_reduce_fusion.1
  464.9 35.8 %all_to_all.72 = bf16[8,128,1280]{2,1,0:T(8,128)(2,1)S(1)} all-to-all(bf16[8,128,1280]{2,1,0:T(8,128)(2,1)S(1)} %broadcast_in_dim.42), channel_id=1, replica_groups=mesh['rep'=16,'tp'=8] {'tp'}, dimensions={0} | all-to-all | bytes 5242880 | tf_op jit(solution)/shard_map/all_to_all | solution.py:39
  500.7 3.8 fusion.25
  504.5 14.4 %convolution_convert_fusion = bf16[1024,1280]{1,0:T(8,128)(2,1)} fusion(bf16[1,1280,640]{2,0,1:T(2,128)(2,1)} %get-tuple-element.20, f32[1024,640]{1,0:T(8,128)} %fusion.25, bf16[1024,1280]{1,0:T(8,128)(2,1)} %bitcast.155, bf16[1,1280,640]{2,0,1:T(2,128)(2,1)} %get-tuple-element.15), kind=kOutput, calls=%fused_computation.8 | convolution fusion | flops 3400007680 | bytes 11141120 | tf_op jit(solution)/shard_map/dot_general | solution.py:129
  518.9 35.4 %all_to_all.73 = bf16[8,128,1280]{2,1,0:T(8,128)(2,1)S(1)} all-to-all(bf16[8,128,1280]{2,1,0:T(8,128)(2,1)} %bitcast.157), channel_id=1, replica_groups=mesh['rep'=16,'tp'=8] {'tp'}, dimensions={0} | all-to-all | bytes 5242880 | tf_op jit(solution)/shard_map/all_to_all | solution.py:62
  554.3 0.4 convert_reduce_fusion
  554.6 0.8 add_convert_fusion
  (74 shorter events, 3.9 us)
Async XLA Ops:
  6.5 84.6 %copy-start = (f32[32,1280]{1,0:T(8,128)S(1)}, f32[32,1280]{1,0:T(8,128)}, u32[]{:S(2)}) copy-start(f32[32,1280]{1,0:T(8,128)} %param.16) | copy-start | bytes 491524
  7.7 15.8 %copy-start.12 = (bf16[2,10,5120]{2,0,1:T(2,128)(2,1)S(1)}, bf16[2,10,5120]{2,0,1:T(2,128)(2,1)}, u32[]{:S(2)}) copy-start(bf16[2,10,5120]{2,0,1:T(2,128)(2,1)} %param.25) | copy-start | bytes 614404
  7.7 15.8 %copy-start.13 = (bf16[2,10,5120]{2,0,1:T(2,128)(2,1)S(1)}, bf16[2,10,5120]{2,0,1:T(2,128)(2,1)}, u32[]{:S(2)}) copy-start(bf16[2,10,5120]{2,0,1:T(2,128)(2,1)} %param.24) | copy-start | bytes 614404
  9.6 13.8 %copy-start.14 = (bf16[2,10,5120]{2,0,1:T(2,128)(2,1)S(1)}, bf16[2,10,5120]{2,0,1:T(2,128)(2,1)}, u32[]{:S(2)}) copy-start(bf16[2,10,5120]{2,0,1:T(2,128)(2,1)} %param.23) | copy-start | bytes 614404
  15.2 29.9 %all-to-all-start.1 = ((bf16[8,2,6400]{2,1,0:T(2,128)(2,1)}), bf16[8,2,6400]{2,1,0:T(2,128)(2,1)S(1)}, u32[]{:S(2)}, u32[]{:S(2)}) async-start(bf16[8,2,6400]{2,1,0:T(2,128)(2,1)} %reshape.234), calls=%async_computation.1 | async-start | bytes 409600 | tf_op jit(solution)/shard_map/all_to_all | solution.py:18
  45.0 6.6 %copy-start.8 = (bf16[8,2,6400]{2,1,0:T(2,128)(2,1)}, bf16[8,2,6400]{2,1,0:T(2,128)(2,1)S(1)}, u32[]{:S(2)}) copy-start(bf16[8,2,6400]{2,1,0:T(2,128)(2,1)S(1)} %all-to-all-done.1) | copy-start | bytes 614404
  45.0 18.0 %all-to-all-start.2 = ((bf16[8,2,19200]{2,1,0:T(2,128)(2,1)}), bf16[8,2,19200]{2,1,0:T(2,128)(2,1)S(1)}, u32[]{:S(2)}, u32[]{:S(2)}) async-start(bf16[8,2,19200]{2,1,0:T(2,128)(2,1)} %reshape.236), calls=%async_computation.2 | async-start | bytes 1228800 | tf_op jit(solution)/shard_map/all_to_all | solution.py:18
  51.7 141.8 %all-gather.2.cloned.1.call-start = ((), (), s32[]{:S(2)}) async-start(), calls=%async_computation.10 | async-start | bytes 13926400 | tf_op jit(solution)/shard_map/all_gather | solution.py:34
  85.1 4.5 copy-start.17
  85.1 4.6 copy-start.18
  85.1 4.7 copy-start.15
  85.1 6.0 %copy-start.11 = (bf16[128,1280]{1,0:T(8,128)(2,1)S(1)}, bf16[128,1280]{1,0:T(8,128)(2,1)}, u32[]{:S(2)}) copy-start(bf16[128,1280]{1,0:T(8,128)(2,1)} %param.13) | copy-start | bytes 983044
  93.6 129.5 %all-to-all-start = ((bf16[8,128,1280]{2,1,0:T(8,128)(2,1)}), bf16[8,128,1280]{2,1,0:T(8,128)(2,1)}, u32[]{:S(2)}, u32[]{:S(2)}) async-start(bf16[8,128,1280]{2,1,0:T(8,128)(2,1)} %broadcast_in_dim.39), calls=%async_computation | async-start | bytes 5242880 | tf_op jit(solution)/shard_map/all_to_all | solution.py:39
  223.1 2.8 copy-start.10
  233.8 1.0 copy-start.7
  237.2 7.4 %copy-start.16 = (f32[2,1280]{1,0:T(2,128)S(1)}, f32[2,1280]{1,0:T(2,128)}, u32[]{:S(2)}) copy-start(f32[2,1280]{1,0:T(2,128)} %param.18) | copy-start | bytes 30724
  237.2 41.0 %all-to-all-start.3 = ((bf16[8,128,1280]{2,1,0:T(8,128)(2,1)}), bf16[8,128,1280]{2,1,0:T(8,128)(2,1)S(1)}, u32[]{:S(2)}, u32[]{:S(2)}) async-start(bf16[8,128,1280]{2,1,0:T(8,128)(2,1)} %bitcast.150), calls=%async_computation.3 | async-start | bytes 5242880 | tf_op jit(solution)/shard_map/all_to_all | solution.py:62
  280.8 37.6 %all-to-all-start.4 = ((bf16[8,128,1280]{2,1,0:T(8,128)(2,1)}), bf16[8,128,1280]{2,1,0:T(8,128)(2,1)}, u32[]{:S(2)}, u32[]{:S(2)}) async-start(bf16[8,128,1280]{2,1,0:T(8,128)(2,1)} %broadcast_in_dim.40), calls=%async_computation.4 | async-start | bytes 5242880 | tf_op jit(solution)/shard_map/all_to_all | solution.py:39
  378.6 36.2 %all-to-all-start.6 = ((bf16[8,128,1280]{2,1,0:T(8,128)(2,1)}), bf16[8,128,1280]{2,1,0:T(8,128)(2,1)}, u32[]{:S(2)}, u32[]{:S(2)}) async-start(bf16[8,128,1280]{2,1,0:T(8,128)(2,1)} %broadcast_in_dim.41), calls=%async_computation.6 | async-start | bytes 5242880 | tf_op jit(solution)/shard_map/all_to_all | solution.py:39
  383.2 7.4 %copy-start.3 = (bf16[1,1280,160]{2,0,1:T(2,128)(2,1)S(1)}, bf16[1,1280,160]{2,0,1:T(2,128)(2,1)}, u32[]{:S(2)}) copy-start(bf16[1,1280,160]{2,0,1:T(2,128)(2,1)} %get-tuple-element.23) | copy-start | bytes 1228804
  383.2 9.9 %copy-start.2 = (bf16[1,1280,160]{2,0,1:T(2,128)(2,1)S(1)}, bf16[1,1280,160]{2,0,1:T(2,128)(2,1)}, u32[]{:S(2)}) copy-start(bf16[1,1280,160]{2,0,1:T(2,128)(2,1)} %get-tuple-element.24) | copy-start | bytes 1228804
  414.8 2.8 copy-start.9
  423.7 1.0 copy-start.6
  464.9 35.8 %copy-start.4 = (bf16[1,1280,640]{2,0,1:T(2,128)(2,1)S(1)}, bf16[1,1280,640]{2,0,1:T(2,128)(2,1)}, u32[]{:S(2)}) copy-start(bf16[1,1280,640]{2,0,1:T(2,128)(2,1)} %get-tuple-element.16) | copy-start | bytes 4915204
  500.7 3.8 copy-start.5
  518.9 36.6 %copy-start.1 = (f32[32,1280]{1,0:T(8,128)S(1)}, f32[32,1280]{1,0:T(8,128)}, u32[]{:S(2)}) copy-start(f32[32,1280]{1,0:T(8,128)} %param.16) | copy-start | bytes 491524
Sparse Core Ops, SparseCore 0:
  89.7 103.7 all-gather.1
where the time goes:
time: 571 us; the launch traced here: 562 us
  waiting for transfers between devices  158 us (28%)
  blocking collectives  146 us (26%)
  local copies, waits for them, and re-layouts  137 us (24%)
  matrix products  60.9 us (11%)
  starting transfers between devices  38.9 us (7%)
  between operations  14.1 us (2%)
  other arithmetic  7.59 us (1%)
    all_to_all x3, blocking collectives, sum_at_owner(): lax.all_to_all(blocks, axis, split_axis=0, concat_axis=0, tiled=True)  110 us
    all_gather x1, waiting for transfers between devices, side_by_side(): lax.all_gather(both, axis, axis=dim, tiled=True)  93 us
    unnamed x52, local copies, waits for them, and re-layouts  60.6 us
    all_to_all x1, blocking collectives, copy_for_each(): lax.all_to_all(jnp.broadcast_to(shard[None], (size, *shard.shape)), axis,...  35.8 us
    all_to_all x1, waiting for transfers between devices, sum_at_owner(): lax.all_to_all(blocks, axis, split_axis=0, concat_axis=0, tiled=True)  33.6 us
    dot_general x4, matrix products, out_terms(): lax.dot_general(mixed_rows, weight, (((1,), (1,)), ((), ())), preferred_e...  32.1 us
    all_to_all x3, waiting for transfers between devices, copy_for_each(): lax.all_to_all(jnp.broadcast_to(shard[None], (size, *shard.shape)), axis,...  31 us
    slice x1, local copies, waits for them, and re-layouts, body(): up_here = up_w[layer_index]  21.6 us
  transfers between devices with their start and end apart: 7, of which 4 were waited for; matrix products, arithmetic and copies ran while one was open for 18% of the time, Pallas kernels for 0%

commit v1 on v0

v1 whole, which is shorter than its diff:
```python
import functools
import math

import jax
import jax.numpy as jnp
import numpy as np
from jax import lax
from jax.experimental import pallas as pl
from jax.experimental.pallas import tpu as pltpu
from jax.sharding import PartitionSpec as P

D = 1280
HEADS = 8
HEAD = 160
VIEWS = 4
HW = 64
LAYERS = 2
ROWS = 128
UNITS = 8
UNIT = 640
MESH = pl.DeviceIdType.MESH
F32 = jnp.float32
BF16 = jnp.bfloat16


def channel_order():
    k = np.arange(D)
    block, rest = k // 80, k % 80
    z, y = block // 4, block % 4
    source, row = rest // 10, rest % 10
    x, core = source // 2, source % 2
    device = (x % 2) * 64 + y * 16 + core * 8 + z * 2 + x // 2
    return (device * 10 + row).astype(np.int32)


def row_packer():
    take = np.zeros((80, 128), np.float32)
    for i in range(80):
        take[i, i // 10 * 16 + i % 10] = 1.0
    return take


def nt_dot(a, b):
    return lax.dot_general(a, b, (((1,), (1,)), ((), ())), preferred_element_type=F32)


def kernel(
    tok_ref,
    aux_ref,
    order_ref,
    take_ref,
    wp_ref,
    out_ref,
    w,
    w2,
    a2a,
    perm,
    aux,
    stream,
    xg,
    mixed,
    hid,
    pst,
    rs,
    wsend,
    wrecv,
    asend,
    arecv,
    gsend,
    grecv,
    rsend,
    rrecv,
):
    r, t = lax.axis_index("rep"), lax.axis_index("tp")
    x = (t % 2) * 2 + r // 8
    y = (r // 2) % 4
    c = r % 2
    z = t // 2
    me8 = x * 2 + c

    def dev(x_, y_, z_, c_):
        return ((x_ % 2) * 8 + y_ * 2 + c_, z_ * 2 + x_ // 2)

    ahead = 1 - 2 * c

    def front(i):
        return (i + ahead + 4) % 4

    def back(i):
        return (i - ahead + 4) % 4

    def opposite(i):
        return (i + 2) % 4

    def slot(x_):
        return (x_ % 2) * 2 + x_ // 2

    x_front, x_back = dev(front(x), y, z, c), dev(back(x), y, z, c)
    y_front, y_back = dev(x, front(y), z, c), dev(x, back(y), z, c)
    z_front, z_back = dev(x, y, front(z), c), dev(x, y, back(z), c)
    partner = dev(x, y, z, 1 - c)

    def other8(offset):
        e = (me8 + offset) % 8
        return e, dev(e // 2, y, z, e % 2)

    barrier = pltpu.get_barrier_semaphore()
    for offset in range(1, 8):
        pl.semaphore_signal(barrier, inc=1, device_id=other8(offset)[1], device_id_type=MESH)
    for d in (y_front, y_back, z_front, z_back):
        pl.semaphore_signal(barrier, inc=1, device_id=d, device_id_type=MESH)
    pl.semaphore_wait(barrier, 11)

    def copy(src, dst, ss, rsem, d):
        return pltpu.make_async_remote_copy(
            src_ref=src, dst_ref=dst, send_sem=ss, recv_sem=rsem, device_id=d, device_id_type=MESH
        )

    def exchange(offset, part):
        e, d = other8(offset)
        if part == 0:
            src, dst = wp_ref.at[e, pl.ds(0, 1)], a2a.at[me8, pl.ds(0, 1)]
        else:
            src, dst = wp_ref.at[e, pl.ds(1, 7)], a2a.at[me8, pl.ds(1, 7)]
        return copy(src, dst, asend.at[offset - 1, part], arecv.at[offset - 1, part], d)

    for part in range(2):
        for offset in range(1, 8):
            exchange(offset, part).start()

    a2a[me8] = wp_ref[me8]

    def unit_rings(u):
        if u % 2 == 0:
            return (y, y_front, y_back), (z, z_front, z_back)
        return (z, z_front, z_back), (y, y_front, y_back)

    def piece(u, i1, i2):
        return w.at[u, i2, i1] if u % 2 == 0 else w.at[u, i1, i2]

    def line(u, i2):
        return w.at[u, i2] if u % 2 == 0 else w.at[u, :, i2]

    def wcopy(u, kind):
        (a, a_front, a_back), (b, b_front, b_back) = unit_rings(u)
        sems = (wsend.at[u, kind], wrecv.at[u, kind])
        if kind == 0:
            return copy(piece(u, a, b), piece(u, a, b), *sems, a_front)
        if kind == 1:
            return copy(piece(u, a, b), piece(u, a, b), *sems, a_back)
        if kind == 2:
            return copy(piece(u, back(a), b), piece(u, back(a), b), *sems, a_front)
        if kind == 3:
            return copy(line(u, b), line(u, b), *sems, b_front)
        if kind == 4:
            return copy(line(u, b), line(u, b), *sems, b_back)
        if kind == 5:
            return copy(line(u, back(b)), line(u, back(b)), *sems, b_front)
        return copy(w.at[u], w2.at[u], *sems, partner)

    def step(u, n):
        if n == 0:
            part = 0 if u == 0 else 1
            if u <= 1:
                for offset in range(1, 8):
                    exchange(offset, part).wait_recv()
            rows = a2a[:, u].reshape(128, UNIT)
            packed = jnp.dot(take_ref[...], rows, preferred_element_type=F32).astype(BF16)
            w[u, z, y] = packed
            wcopy(u, 0).start()
            wcopy(u, 1).start()
        elif n == 1:
            wcopy(u, 0).wait_recv()
            wcopy(u, 2).start()
        elif n == 2:
            wcopy(u, 1).wait_recv()
            wcopy(u, 2).wait_recv()
            wcopy(u, 3).start()
            wcopy(u, 4).start()
        elif n == 3:
            wcopy(u, 3).wait_recv()
            wcopy(u, 5).start()
        elif n == 4:
            wcopy(u, 4).wait_recv()
            wcopy(u, 5).wait_recv()
            wcopy(u, 6).start()

    todo = []
    for tick in range(UNITS + 5):
        for n in range(4, -1, -1):
            u = tick - n
            if 0 <= u < UNITS:
                todo.append((u, n))
    ready = set()

    def pump(count):
        for _ in range(min(count, len(todo))):
            step(*todo.pop(0))

    def need(u):
        while (u, 4) in todo:
            pump(1)
        if u not in ready:
            wcopy(u, 6).wait_recv()
            ready.add(u)

    pump(3)

    perm[...] = (
        lax.broadcasted_iota(jnp.int32, (D, D), 0) == order_ref[...]
    ).astype(F32).astype(BF16)
    rows = aux_ref[...]
    high = rows.astype(BF16)
    left = rows - high.astype(F32)
    middle = left.astype(BF16)
    low = (left - middle.astype(F32)).astype(BF16)
    aux[...] = (
        jnp.dot(high, perm[...], preferred_element_type=F32)
        + jnp.dot(middle, perm[...], preferred_element_type=F32)
        + jnp.dot(low, perm[...], preferred_element_type=F32)
    )
    tokens = jnp.dot(tok_ref[...], perm[...], preferred_element_type=F32)
    stream[0:HW, :] = tokens[0:HW, :] + aux[0:1, :]
    stream[HW : 2 * HW, :] = tokens[HW : 2 * HW, :] + aux[1:2, :]

    def gather_start(gain):
        rows = stream[...]
        mean = jnp.mean(rows, axis=-1, keepdims=True)
        centred = rows - mean
        spread = jnp.mean(centred * centred, axis=-1, keepdims=True)
        xg[slot(x)] = (centred * lax.rsqrt(spread + 1e-05) * gain).astype(BF16)
        gcopy(0).start()
        gcopy(1).start()

    def gcopy(kind):
        sems = (gsend.at[kind], grecv.at[kind])
        if kind == 0:
            return copy(xg.at[slot(x)], xg.at[slot(x)], *sems, x_front)
        if kind == 1:
            return copy(xg.at[slot(x)], xg.at[slot(x)], *sems, x_back)
        return copy(xg.at[slot(back(x))], xg.at[slot(back(x))], *sems, x_front)

    def gather_finish():
        gcopy(0).wait_recv()
        gcopy(2).start()
        pump(2)
        gcopy(1).wait_recv()
        gcopy(2).wait_recv()
        for kind in range(3):
            gcopy(kind).wait_send()

    def rcopy(kind):
        target = x_back if kind == 1 else x_front
        return copy(pst.at[kind], rs.at[kind], rsend.at[kind], rrecv.at[kind], target)

    def reduce(partial):
        pst[0] = partial(slot(opposite(x))).astype(BF16)
        rcopy(0).start()
        pst[1] = partial(slot(back(x))).astype(BF16)
        rcopy(1).start()
        mine = partial(slot(front(x)))
        pump(2)
        rcopy(0).wait_recv()
        pst[2] = (mine + rs[0].astype(F32)).astype(BF16)
        rcopy(2).start()
        mine = partial(slot(x))
        stream[...] += mine
        pump(2)
        rcopy(1).wait_recv()
        rcopy(2).wait_recv()
        stream[...] += rs[1].astype(F32) + rs[2].astype(F32)
        for kind in range(3):
            rcopy(kind).wait_send()

    lane = lax.broadcasted_iota(jnp.int32, (256, 256), 1)

    for layer in range(LAYERS):
        attn_u, gate_u, up_u, down_u = (4 * layer + i for i in range(4))
        gather_start(aux[2 + layer : 3 + layer, :])
        need(attn_u)
        gather_finish()
        for half, held in enumerate((w, w2)):
            for pair in range(2):
                rows = xg[2 * pair : 2 * pair + 2].reshape(256, D)
                packed = jnp.dot(
                    rows, held[attn_u, :, :, :, 0:512].reshape(D, 512), preferred_element_type=F32
                )
                query = jnp.where(lane < HEAD, packed[:, 0:256], 0.0).astype(BF16)
                key = pltpu.roll(packed[:, 128:384], 224, 1).astype(BF16)
                value = jnp.where(lane >= 96, pltpu.roll(packed[:, 256:512], 32, 1), 0.0).astype(BF16)
                scores = nt_dot(query, key) * HEAD ** (-0.5)
                peak = jnp.max(scores, axis=-1, keepdims=True)
                expons = jnp.exp(scores - peak)
                probs = (expons / jnp.sum(expons, axis=-1, keepdims=True)).astype(BF16)
                heads = jnp.dot(probs, value, preferred_element_type=F32).astype(BF16)
                mixed[half, 2 * pair : 2 * pair + 2] = heads.reshape(2, ROWS, 256)

        def attn_partial(s):
            total = nt_dot(mixed[0, s], w[attn_u, :, :, :, 384:640].reshape(D, 256))
            return total + nt_dot(mixed[1, s], w2[attn_u, :, :, :, 384:640].reshape(D, 256))

        reduce(attn_partial)
        gather_start(aux[4 + layer : 5 + layer, :])
        need(gate_u)
        need(up_u)
        gather_finish()
        rows = xg[...].reshape(4 * ROWS, D)
        for half, held in enumerate((w, w2)):
            for j in range(5):
                cols = slice(128 * j, 128 * j + 128)
                both = jnp.concatenate(
                    [
                        held[gate_u, :, :, :, cols].reshape(D, 128),
                        held[up_u, :, :, :, cols].reshape(D, 128),
                    ],
                    axis=1,
                )
                packed = jnp.dot(rows, both, preferred_element_type=F32)
                gate = packed[:, 0:128]
                act = 0.5 * gate * (1.0 + lax.erf(gate * math.sqrt(0.5)))
                hid[half, :, :, cols] = (act * packed[:, 128:256]).astype(BF16).reshape(4, ROWS, 128)
        need(down_u)

        def ffn_partial(s):
            total = nt_dot(hid[0, s], w[down_u].reshape(D, UNIT))
            return total + nt_dot(hid[1, s], w2[down_u].reshape(D, UNIT))

        reduce(ffn_partial)

    out_ref[...] = nt_dot(stream[...].astype(BF16), perm[...]).astype(BF16)

    for part in range(2):
        for offset in range(1, 8):
            exchange(offset, part).wait_send()
    for u in range(UNITS):
        for kind in range(7):
            wcopy(u, kind).wait_send()


def conditioning(view_ids, time_ids, camera_table):
    t = lax.axis_index("tp")
    views = lax.dynamic_slice(view_ids, (t // 2, t % 2 * 2), (1, 2)).reshape(2)
    step = lax.dynamic_slice(time_ids, (t // 2,), (1,))
    half = D // 2
    frequency = jnp.exp(-math.log(10000.0) * jnp.arange(half, dtype=F32) / half)
    angles = step.astype(F32)[:, None] * frequency[None, :]
    code = jnp.concatenate([jnp.cos(angles), jnp.sin(angles)], axis=1)
    return camera_table[views] + code


def send_layout(weights):
    small = [a.reshape(2, 10, 8, HEAD) for a in weights[:4]]
    attn = jnp.concatenate(small, axis=3)[:, None]
    big = [a.reshape(2, 10, 8, UNIT)[:, None] for a in weights[4:]]
    units = jnp.concatenate([attn, *big], axis=1)
    units = units.transpose(3, 0, 1, 2, 4).reshape(8, UNITS, 10, UNIT)
    return jnp.pad(units, ((0, 0), (0, 0), (0, 6), (0, 0)))


def body(tokens, view_ids, time_ids, camera_table, norm_attn, norm_ffn, *weights):
    cond = conditioning(view_ids, time_ids, camera_table)
    aux = jnp.concatenate([cond, norm_attn, norm_ffn, jnp.zeros((2, D), F32)], axis=0)
    order = jnp.asarray(channel_order())[None, :]
    take = jnp.asarray(row_packer(), BF16)
    vmem = pl.BlockSpec(memory_space=pltpu.VMEM)
    dma = pltpu.SemaphoreType.DMA
    return pl.pallas_call(
        kernel,
        out_shape=jax.ShapeDtypeStruct((ROWS, D), BF16),
        in_specs=[vmem] * 5,
        out_specs=vmem,
        scratch_shapes=[
            pltpu.VMEM((UNITS, 4, 4, 80, UNIT), BF16),
            pltpu.VMEM((UNITS, 4, 4, 80, UNIT), BF16),
            pltpu.VMEM((8, UNITS, 16, UNIT), BF16),
            pltpu.VMEM((D, D), BF16),
            pltpu.VMEM((8, D), F32),
            pltpu.VMEM((ROWS, D), F32),
            pltpu.VMEM((4, ROWS, D), BF16),
            pltpu.VMEM((2, 4, ROWS, 256), BF16),
            pltpu.VMEM((2, 4, ROWS, UNIT), BF16),
            pltpu.VMEM((3, ROWS, D), BF16),
            pltpu.VMEM((3, ROWS, D), BF16),
            dma((UNITS, 7)),
            dma((UNITS, 7)),
            dma((7, 2)),
            dma((7, 2)),
            dma((3,)),
            dma((3,)),
            dma((3,)),
            dma((3,)),
        ],
        compiler_params=pltpu.CompilerParams(
            collective_id=0, has_side_effects=True, vmem_limit_bytes=60 * 1024 * 1024
        ),
    )(tokens, aux, order, take, send_layout(weights))


def solution(mesh):
    return jax.shard_map(
        body,
        mesh=mesh,
        in_specs=(
            P(("rep", "tp"), None),
            P("rep", None),
            P("rep"),
            P(),
            P(),
            P(),
            *([P(None, ("rep", "tp"), None)] * 7),
        ),
        out_specs=P(("rep", "tp"), None),
        check_vma=False,
    )
```

time: 571 us -> 196 us (0.34)
  Pallas kernels: 0 us -> 180 us
  waiting for transfers between devices: 158 us -> 0 us
  blocking collectives: 146 us -> 0 us
  local copies, waits for them, and re-layouts: 137 us -> 8.79 us
  matrix products: 60.9 us -> 0 us
  starting transfers between devices: 38.9 us -> 0 us
  between operations: 14.1 us -> 0.86 us
    pallas_call x0 -> x1, Pallas kernels: none -> 180 us  [body(): pl.pallas_call(kernel, out_shape=jax.ShapeDtypeStruct((ROWS, D), BF16), i...]
    all_to_all x4 -> x0, blocking collectives: 146 us -> none  [the longest x3 110 us: sum_at_owner(): lax.all_to_all(blocks, axis, split_axis=0, concat_axis=0, tiled=True)]
    all_gather x1 -> x0, waiting for transfers between devices: 93 us -> none  [side_by_side(): lax.all_gather(both, axis, axis=dim, tiled=True)]
    all_to_all x6 -> x0, waiting for transfers between devices: 64.6 us -> none  [the longest x1 33.6 us: sum_at_owner(): lax.all_to_all(blocks, axis, split_axis=0, concat_axis=0, tiled=True)]
    dot_general x15 -> x0, matrix products: 59.8 us -> none  [the longest x4 32.1 us: out_terms(): lax.dot_general(mixed_rows, weight, (((1,), (1,)), ((), ())), preferred_e...]
    unnamed x52 -> x11, local copies, waits for them, and re-layouts: 60.6 us -> 1.99 us
    slice x6 -> x0, local copies, waits for them, and re-layouts: 43.9 us -> none  [the longest x1 21.6 us: body(): up_here = up_w[layer_index]]
    all_to_all x6 -> x0, starting transfers between devices: 38.7 us -> none  [the longest x3 16.3 us: copy_for_each(): lax.all_to_all(jnp.broadcast_to(shard[None], (size, *shard.shape)), axis,...]
  transfers between devices with their start and end apart: 7 -> 0, of which waited for: 4 -> 0; matrix products, arithmetic and copies ran while one was open for 18% -> 0% of each run, Pallas kernels for 0% -> 0%
where the time goes in v1:
time: 196 us; the launch traced here: 193 us
  Pallas kernels  180 us (92%)
  local copies, waits for them, and re-layouts  8.79 us (4%)
  other arithmetic  2.85 us (1%)
    pallas_call x1, Pallas kernels, body(): pl.pallas_call(kernel, out_shape=jax.ShapeDtypeStruct((ROWS, D), BF16), i...  180 us

profile of v1, /device:TPU:1, one launch (start us, length us, event | category | flops | bytes accessed | tf_op | source)
XLA Modules:
  0.0 193.0 jit_solution(8869457230884626407)
XLA Ops:
  0.0 0.0 copy-start
  0.0 0.0 copy-start.1
  0.0 0.0 copy-start.4
  0.0 1.3 dynamic_slice.7
  2.0 0.8 fusion.2
  2.7 0.1 pad.16.clone
  2.8 0.1 fusion
  3.0 0.0 copy-done
  3.0 0.6 gather_fusion
  3.6 1.4 maximum_maximum_fusion.aux_ref
  5.0 0.9 reshape.73
  5.9 0.9 reshape.74
  6.9 0.0 copy-start.2
  6.9 1.0 reshape.75
  8.0 0.0 copy-done.4
  8.0 0.1 reshape.76
  8.1 0.0 copy-start.3
  8.1 0.3 maximum_bitcast_fusion
  8.4 0.0 copy-done.1
  8.4 0.1 broadcast_in_dim_reshape.9
  8.6 0.1 copy.20
  8.6 0.0 copy-done.2
  8.6 0.1 broadcast_in_dim_reshape.10
  8.8 0.1 copy.21
  8.8 0.3 copy-done.3
  9.1 0.1 broadcast_in_dim_reshape.11
  9.2 0.1 copy.22
  9.3 0.3 pad_maximum_fusion
  9.6 1.2 pad.4.wp_ref
  10.8 180.5 %shard_map.145 = bf16[128,1280]{1,0:T(8,128)(2,1)} custom-call(bf16[128,1280]{1,0:T(8,128)(2,1)} %tok_ref.1, f32[8,1280]{1,0:T(8,128)} %maximum_maximum_fusion.aux_ref, s32[1,1280]{1,0:T(1,128)} %constant.63.order_ref, bf16[80,128]{1,0:T(8,128)(2,1)} %constant.51.clone.take_ref, bf16[8,8,16,640]{3,2,1,0:T(8,128)(2,1)} %pad.4.wp_ref), custom_call_target="tpu_custom_call" | custom-call | tf_op jit(solution)/shard_map/pallas_call | solution.py:367
  191.3 1.7 copy.24
  (8 shorter events, 0.2 us)
Async XLA Ops:
  0.0 3.0 %copy-start = (f32[32,1280]{1,0:T(8,128)S(1)}, f32[32,1280]{1,0:T(8,128)}, u32[]{:S(2)}) copy-start(f32[32,1280]{1,0:T(8,128)} %param.18) | copy-start | bytes 491524
  0.0 8.4 %copy-start.1 = (bf16[2,10,5120]{2,0,1:T(2,128)(2,1)S(1)}, bf16[2,10,5120]{2,0,1:T(2,128)(2,1)}, u32[]{:S(2)}) copy-start(bf16[2,10,5120]{2,0,1:T(2,128)(2,1)} %param.25) | copy-start | bytes 614404
  0.0 7.9 %copy-start.4 = (bf16[2,10,1280]{2,0,1:T(2,128)(2,1)S(1)}, bf16[2,10,1280]{2,0,1:T(2,128)(2,1)}, u32[]{:S(2)}) copy-start(bf16[2,10,1280]{2,0,1:T(2,128)(2,1)} %param.24) | copy-start | bytes 153604
  6.9 1.7 copy-start.2
  8.1 0.9 copy-start.3

commit v2 on v1

v2 whole, which is shorter than its diff:
```python
import functools
import math

import jax
import jax.numpy as jnp
import numpy as np
from jax import lax
from jax.experimental import pallas as pl
from jax.experimental.pallas import tpu as pltpu
from jax.sharding import PartitionSpec as P

D = 1280
HEADS = 8
HEAD = 160
VIEWS = 4
HW = 64
LAYERS = 2
ROWS = 128
UNITS = 8
UNIT = 640
MESH = pl.DeviceIdType.MESH
F32 = jnp.float32
BF16 = jnp.bfloat16


def channel_order():
    k = np.arange(D)
    block, rest = k // 80, k % 80
    z, y = block // 4, block % 4
    source, row = rest // 10, rest % 10
    x, core = source // 2, source % 2
    device = (x % 2) * 64 + y * 16 + core * 8 + z * 2 + x // 2
    return (device * 10 + row).astype(np.int32)


def row_sorter():
    take = np.zeros((160, 160), np.float32)
    for layer in range(2):
        for i in range(80):
            take[layer * 80 + i, i * 2 + layer] = 1.0
    return take


def nt_dot(a, b):
    return lax.dot_general(a, b, (((1,), (1,)), ((), ())), preferred_element_type=F32)


def kernel(
    tok_ref,
    view_ref,
    time_ref,
    table_ref,
    norm_attn_ref,
    norm_ffn_ref,
    order_ref,
    sort_ref,
    wq_ref,
    wk_ref,
    wv_ref,
    wo_ref,
    wg_ref,
    wu_ref,
    wd_ref,
    out_ref,
    w,
    w2,
    a2a,
    parts,
    perm,
    raw,
    aux,
    stream,
    xg,
    queries,
    keys,
    values,
    mixed,
    hid,
    terms,
    pst,
    rs,
    wsend,
    wrecv,
    asend,
    arecv,
    lsem,
    gsend,
    grecv,
    rsend,
    rrecv,
):
    r, t = lax.axis_index("rep"), lax.axis_index("tp")
    x = (t % 2) * 2 + r // 8
    y = (r // 2) % 4
    c = r % 2
    z = t // 2
    me8 = x * 2 + c

    def dev(x_, y_, z_, c_):
        return ((x_ % 2) * 8 + y_ * 2 + c_, z_ * 2 + x_ // 2)

    ahead = 1 - 2 * c

    def front(i):
        return (i + ahead + 4) % 4

    def back(i):
        return (i - ahead + 4) % 4

    def opposite(i):
        return (i + 2) % 4

    def slot(x_):
        return (x_ % 2) * 2 + x_ // 2

    x_front, x_back = dev(front(x), y, z, c), dev(back(x), y, z, c)
    y_front, y_back = dev(x, front(y), z, c), dev(x, back(y), z, c)
    z_front, z_back = dev(x, y, front(z), c), dev(x, y, back(z), c)
    partner = dev(x, y, z, 1 - c)

    def other8(offset):
        e = (me8 + offset) % 8
        return e, dev(e // 2, y, z, e % 2)

    barrier = pltpu.get_barrier_semaphore()
    for offset in range(1, 8):
        pl.semaphore_signal(barrier, inc=1, device_id=other8(offset)[1], device_id_type=MESH)
    for d in (y_front, y_back, z_front, z_back):
        pl.semaphore_signal(barrier, inc=1, device_id=d, device_id_type=MESH)

    rows = [ref[...].astype(F32) for ref in (wq_ref, wk_ref, wv_ref, wo_ref)]
    for e in range(8):
        cut = [a[:, :, HEAD * e : HEAD * e + HEAD] for a in rows]
        parts[e] = jnp.concatenate(cut, axis=2).astype(BF16)

    perm[...] = (
        lax.broadcasted_iota(jnp.int32, (D, D), 0) == order_ref[...]
    ).astype(F32).astype(BF16)
    frequency = jnp.exp(
        lax.broadcasted_iota(jnp.int32, (1, D // 2), 1).astype(F32) * (-math.log(10000.0) / (D // 2))
    )
    angles = time_ref[t // 2].astype(F32) * frequency
    code = jnp.concatenate([jnp.cos(angles), jnp.sin(angles)], axis=1)
    for v in range(2):
        pose = view_ref[t // 2, (t % 2) * 2 + v]
        raw[v : v + 1, :] = table_ref[pl.ds(pose, 1), :] + code
    raw[2:4, :] = norm_attn_ref[...]
    raw[4:6, :] = norm_ffn_ref[...]
    raw[6:8, :] = jnp.zeros((2, D), F32)
    rows = raw[...]
    high = rows.astype(BF16)
    left = rows - high.astype(F32)
    middle = left.astype(BF16)
    low = (left - middle.astype(F32)).astype(BF16)
    aux[...] = (
        jnp.dot(high, perm[...], preferred_element_type=F32)
        + jnp.dot(middle, perm[...], preferred_element_type=F32)
        + jnp.dot(low, perm[...], preferred_element_type=F32)
    )
    tokens = jnp.dot(tok_ref[...], perm[...], preferred_element_type=F32)
    for h in range(2):
        stream[h] = tokens[HW * h : HW * h + HW, :] + aux[h : h + 1, :]

    pl.semaphore_wait(barrier, 11)

    def copy(src, dst, ss, rsem, d):
        return pltpu.make_async_remote_copy(
            src_ref=src, dst_ref=dst, send_sem=ss, recv_sem=rsem, device_id=d, device_id_type=MESH
        )

    def shard(e, part):
        if part == 0:
            return parts.at[e]
        ref = (wg_ref, wu_ref, wd_ref)[part - 1]
        return ref.at[:, :, pl.ds(pl.multiple_of(e * UNIT, UNIT), UNIT)]

    def exchange(offset, part):
        e, d = other8(offset)
        sems = (asend.at[offset - 1, part], arecv.at[offset - 1, part])
        return copy(shard(e, part), a2a.at[part, me8], *sems, d)

    def keep(part):
        return pltpu.make_async_copy(shard(me8, part), a2a.at[part, me8], lsem.at[part])

    for part in range(4):
        for offset in range(1, 8):
            exchange(offset, part).start()
        keep(part).start()

    def rings(h):
        if h == 0:
            return (y, y_front, y_back), (z, z_front, z_back)
        return (z, z_front, z_back), (y, y_front, y_back)

    def lanes(u, h):
        cut = 384 if u % 2 == 0 else 256
        return pl.ds(0, cut) if h == 0 else pl.ds(cut, UNIT - cut)

    def piece(ref, u, h, i1, i2):
        return ref.at[u, i2, i1, :, lanes(u, h)] if h == 0 else ref.at[u, i1, i2, :, lanes(u, h)]

    def line(ref, u, h, i2):
        return ref.at[u, i2, :, :, lanes(u, h)] if h == 0 else ref.at[u, :, i2, :, lanes(u, h)]

    def wcopy(u, h, kind):
        (a, a_front, a_back), (b, b_front, b_back) = rings(h)
        sems = (wsend.at[u, h, kind], wrecv.at[u, h, kind])
        if kind < 3:
            held = piece(w, u, h, back(a) if kind == 2 else a, b)
            return copy(held, held, *sems, a_back if kind == 1 else a_front)
        if kind < 6:
            held = line(w, u, h, back(b) if kind == 5 else b)
            return copy(held, held, *sems, b_back if kind == 4 else b_front)
        at = (b, back(b), front(b), opposite(b))[kind - 6]
        return copy(line(w, u, h, at), line(w2, u, h, at), *sems, partner)

    def step(u, n):
        if n == 0:
            if u < 4:
                keep(u).wait()
                for offset in range(1, 8):
                    exchange(offset, u).wait_recv()
                sorted_rows = jnp.dot(sort_ref[...], a2a[u].reshape(160, UNIT), preferred_element_type=F32)
                w[u, z, y] = sorted_rows[0:80].astype(BF16)
                w[u + 4, z, y] = sorted_rows[80:160].astype(BF16)
        for h in range(2):
            if n == 0:
                wcopy(u, h, 0).start()
                wcopy(u, h, 1).start()
            elif n == 1:
                wcopy(u, h, 0).wait_recv()
                wcopy(u, h, 2).start()
            elif n == 2:
                wcopy(u, h, 1).wait_recv()
                wcopy(u, h, 2).wait_recv()
                wcopy(u, h, 3).start()
                wcopy(u, h, 4).start()
                wcopy(u, h, 6).start()
            elif n == 3:
                wcopy(u, h, 3).wait_recv()
                wcopy(u, h, 5).start()
                wcopy(u, h, 7).start()
            elif n == 4:
                wcopy(u, h, 4).wait_recv()
                wcopy(u, h, 8).start()
            elif n == 5:
                wcopy(u, h, 5).wait_recv()
                wcopy(u, h, 9).start()

    first = [(0, 0), (0, 1), (1, 0), (0, 2), (1, 1), (2, 0), (0, 3), (1, 2), (2, 1), (3, 0), (0, 4), (0, 5)]

    def due(u, n):
        while n < 3:
            u, n = u - 1, n + 1
        return 6.5 + 9.3 * (u - 1) + (0.0, 5.0, 5.5)[n - 3]

    later = [(u, n) for u in range(UNITS) for n in range(6) if (u, n) not in first]
    later.sort(key=lambda item: (due(*item), -item[1]))
    todo = [(-1.0, u, n) for u, n in first] + [(due(u, n), u, n) for u, n in later]
    ready = set()

    def advance():
        _, u, n = todo.pop(0)
        with jax.named_scope(f"pump_{u}_{n}"):
            step(u, n)

    def pump(now):
        while todo and todo[0][0] <= now:
            advance()

    def need(u):
        while any(item[1:] == (u, 5) for item in todo):
            advance()
        if u not in ready:
            with jax.named_scope(f"need_{u}"):
                for h in range(2):
                    for kind in range(6, 10):
                        wcopy(u, h, kind).wait_recv()
            ready.add(u)

    def gather_start(h, gain):
        rows = stream[h]
        mean = jnp.mean(rows, axis=-1, keepdims=True)
        centred = rows - mean
        spread = jnp.mean(centred * centred, axis=-1, keepdims=True)
        xg[h, slot(x)] = (centred * lax.rsqrt(spread + 1e-05) * gain).astype(BF16)
        gcopy(h, 0).start()
        gcopy(h, 1).start()

    def gcopy(h, kind):
        held = xg.at[h, slot(back(x) if kind == 2 else x)]
        return copy(held, held, gsend.at[h, kind], grecv.at[h, kind], x_back if kind == 1 else x_front)

    def gather_forward(h):
        gcopy(h, 0).wait_recv()
        gcopy(h, 2).start()

    def gather_finish(h):
        gcopy(h, 1).wait_recv()
        gcopy(h, 2).wait_recv()
        for kind in range(3):
            gcopy(h, kind).wait_send()

    def rcopy(h, kind):
        target = x_back if kind == 1 else x_front
        return copy(pst.at[h, kind], rs.at[h, kind], rsend.at[h, kind], rrecv.at[h, kind], target)

    def reduce_start(h, partial):
        terms[h] = partial(h).reshape(4, HW, D)
        pst[h, 0] = terms[h, slot(opposite(x))].astype(BF16)
        rcopy(h, 0).start()
        pst[h, 1] = terms[h, slot(back(x))].astype(BF16)
        rcopy(h, 1).start()

    def reduce_forward(h):
        rcopy(h, 0).wait_recv()
        pst[h, 2] = (terms[h, slot(front(x))] + rs[h, 0].astype(F32)).astype(BF16)
        rcopy(h, 2).start()

    def reduce_finish(h):
        mine = stream[h] + terms[h, slot(x)]
        rcopy(h, 1).wait_recv()
        rcopy(h, 2).wait_recv()
        stream[h] = mine + (rs[h, 1].astype(F32) + rs[h, 2].astype(F32))
        for kind in range(3):
            rcopy(h, kind).wait_send()

    lane = lax.broadcasted_iota(jnp.int32, (256, 256), 1)

    def project(h, u):
        rows = xg[h].reshape(256, D)
        for half, held in enumerate((w, w2)):
            packed = jnp.dot(rows, held[u, :, :, :, 0:512].reshape(D, 512), preferred_element_type=F32)
            query = jnp.where(lane < HEAD, packed[:, 0:256], 0.0)
            key = pltpu.roll(packed[:, 128:384], 224, 1)
            value = jnp.where(lane >= 96, pltpu.roll(packed[:, 256:512], 32, 1), 0.0)
            queries[half, h] = query.astype(BF16).reshape(2, 128, 256)
            keys[half, :, h] = key.astype(BF16).reshape(2, 128, 256)
            values[half, :, h] = value.astype(BF16).reshape(2, 128, 256)

    def attend(h):
        for half in range(2):
            for pair in range(2):
                scores = nt_dot(queries[half, h, pair], keys[half, pair].reshape(256, 256))
                scores = scores * HEAD ** (-0.5)
                peak = jnp.max(scores, axis=-1, keepdims=True)
                expons = jnp.exp(scores - peak)
                probs = (expons / jnp.sum(expons, axis=-1, keepdims=True)).astype(BF16)
                heads = jnp.dot(probs, values[half, pair].reshape(256, 256), preferred_element_type=F32)
                mixed[half, h, pair] = heads.astype(BF16)

    def feed(h, gate_u, up_u, now):
        rows = xg[h].reshape(256, D)
        for half, held in enumerate((w, w2)):
            pump(now + 1.4 * half)
            for j in range(5):
                cols = slice(128 * j, 128 * j + 128)
                both = jnp.concatenate(
                    [
                        held[gate_u, :, :, :, cols].reshape(D, 128),
                        held[up_u, :, :, :, cols].reshape(D, 128),
                    ],
                    axis=1,
                )
                packed = jnp.dot(rows, both, preferred_element_type=F32)
                gate = packed[:, 0:128]
                act = 0.5 * gate * (1.0 + lax.erf(gate * math.sqrt(0.5)))
                hid[half, h, :, cols] = (act * packed[:, 128:256]).astype(BF16)

    for _ in range(3):
        advance()
    for h in range(2):
        gather_start(h, aux[2:3, :])
    for layer in range(LAYERS):
        attn_u, gate_u, up_u, down_u = (4 * layer + i for i in range(4))
        base = 48 * layer

        def attn_partial(h):
            total = nt_dot(
                mixed[0, h].reshape(256, 256), w[attn_u, :, :, :, 384:640].reshape(D, 256)
            )
            return total + nt_dot(
                mixed[1, h].reshape(256, 256), w2[attn_u, :, :, :, 384:640].reshape(D, 256)
            )

        def ffn_partial(h):
            total = nt_dot(hid[0, h], w[down_u].reshape(D, UNIT))
            return total + nt_dot(hid[1, h], w2[down_u].reshape(D, UNIT))

        def both_reduced(gain, now):
            for h in range(2):
                reduce_forward(h)
                pump(now + 4.5 + 2 * h)
            for h in range(2):
                reduce_finish(h)
                if gain is not None:
                    gather_start(h, gain)
                pump(now + 10 + 3.5 * h)

        need(attn_u)
        pump(base)
        for h in range(2):
            gather_forward(h)
            pump(base + 2 + 2 * h)
        for h in range(2):
            gather_finish(h)
            project(h, attn_u)
            pump(base + 5.5 + 1.5 * h)
        for h in range(2):
            attend(h)
            pump(base + 8 + 1.7 * h)
            reduce_start(h, attn_partial)
            pump(base + 8.8 + 1.7 * h)
        both_reduced(aux[4 + layer : 5 + layer, :], base + 10.5)
        for h in range(2):
            gather_forward(h)
            pump(base + 27 + 2.5 * h)
        need(gate_u)
        need(up_u)
        for h in range(2):
            gather_finish(h)
            feed(h, gate_u, up_u, base + 31.5 + 4 * h)
            if h == 0:
                need(down_u)
            pump(base + 34 + 4 * h)
            reduce_start(h, ffn_partial)
            pump(base + 35.3 + 4 * h)
        both_reduced(aux[3:4, :] if layer == 0 else None, base + 39)

    for h in range(2):
        out_ref[HW * h : HW * h + HW, :] = nt_dot(stream[h].astype(BF16), perm[...]).astype(BF16)

    for part in range(4):
        for offset in range(1, 8):
            exchange(offset, part).wait_send()
    for u in range(UNITS):
        for h in range(2):
            for kind in range(10):
                wcopy(u, h, kind).wait_send()


def body(tokens, view_ids, time_ids, camera_table, norm_attn, norm_ffn, *weights):
    order = jnp.asarray(channel_order())[None, :]
    sorter = jnp.asarray(row_sorter(), BF16)
    weights = [a.transpose(1, 0, 2) for a in weights]
    vmem = pl.BlockSpec(memory_space=pltpu.VMEM)
    smem = pl.BlockSpec(memory_space=pltpu.SMEM)
    dma = pltpu.SemaphoreType.DMA
    return pl.pallas_call(
        kernel,
        out_shape=jax.ShapeDtypeStruct((ROWS, D), BF16),
        in_specs=[vmem, smem, smem] + [vmem] * 9 + [pl.BlockSpec(memory_space=pl.ANY)] * 3,
        out_specs=vmem,
        scratch_shapes=[
            pltpu.VMEM((UNITS, 4, 4, 80, UNIT), BF16),
            pltpu.VMEM((UNITS, 4, 4, 80, UNIT), BF16),
            pltpu.VMEM((4, 8, 10, LAYERS, UNIT), BF16),
            pltpu.VMEM((8, 10, LAYERS, UNIT), BF16),
            pltpu.VMEM((D, D), BF16),
            pltpu.VMEM((8, D), F32),
            pltpu.VMEM((8, D), F32),
            pltpu.VMEM((2, HW, D), F32),
            pltpu.VMEM((2, 4, HW, D), BF16),
            pltpu.VMEM((2, 2, 2, 128, 256), BF16),
            pltpu.VMEM((2, 2, 2, 128, 256), BF16),
            pltpu.VMEM((2, 2, 2, 128, 256), BF16),
            pltpu.VMEM((2, 2, 2, 128, 256), BF16),
            pltpu.VMEM((2, 2, 256, UNIT), BF16),
            pltpu.VMEM((2, 4, HW, D), F32),
            pltpu.VMEM((2, 3, HW, D), BF16),
            pltpu.VMEM((2, 3, HW, D), BF16),
            dma((UNITS, 2, 10)),
            dma((UNITS, 2, 10)),
            dma((7, 4)),
            dma((7, 4)),
            dma((4,)),
            dma((2, 3)),
            dma((2, 3)),
            dma((2, 3)),
            dma((2, 3)),
        ],
        compiler_params=pltpu.CompilerParams(
            collective_id=0, has_side_effects=True, vmem_limit_bytes=60 * 1024 * 1024
        ),
    )(tokens, view_ids, time_ids, camera_table, norm_attn, norm_ffn, order, sorter, *weights)


def solution(mesh):
    return jax.shard_map(
        body,
        mesh=mesh,
        in_specs=(
            P(("rep", "tp"), None),
            P("rep", None),
            P("rep"),
            P(),
            P(),
            P(),
            *([P(None, ("rep", "tp"), None)] * 7),
        ),
        out_specs=P(("rep", "tp"), None),
        check_vma=False,
    )
```

time: 196 us -> 148 us (0.76); the launches traced: 193 us -> 148 us
  Pallas kernels: 180 us -> 146 us
  local copies, waits for them, and re-layouts: 8.79 us -> 1.72 us
  other arithmetic: 2.85 us -> 0 us
    pallas_call x1, Pallas kernels: 180 us -> 146 us  [body(): pl.pallas_call(kernel, out_shape=jax.ShapeDtypeStruct((ROWS, D), BF16), i...]
    reshape x8 -> x0, local copies, waits for them, and re-layouts: 3.11 us -> none  [send_layout(): small = [a.reshape(2, 10, 8, HEAD) for a in weights[:4]]]
where the time goes in v2:
time: 148 us
  Pallas kernels  146 us (99%)
  local copies, waits for them, and re-layouts  1.72 us (1%)
    pallas_call x1, Pallas kernels, body(): pl.pallas_call(kernel, out_shape=jax.ShapeDtypeStruct((ROWS, D), BF16), i...  146 us

profile of v2, /device:TPU:1, one launch (start us, length us, event | category | flops | bytes accessed | tf_op | source)
XLA Modules:
  0.0 147.7 jit_solution(10133339762321811424)
XLA Ops:
  0.0 146.0 %shard_map.145 = bf16[128,1280]{1,0:T(8,128)(2,1)} custom-call(bf16[128,1280]{1,0:T(8,128)(2,1)} %tok_ref.1, s32[4,4]{1,0:T(4,128)} %view_ref.1, s32[4]{0:T(128)} %time_ref.1, f32[32,1280]{1,0:T(8,128)} %table_ref.1, f32[2,1280]{1,0:T(2,128)} %norm_attn_ref.1, f32[2,1280]{1,0:T(2,128)} %norm_ffn_ref.1, s32[1,1280]{1,0:T(1,128)} %constant.15.order_ref, ...), custom_call_target="tpu_custom_call" | custom-call | tf_op jit(solution)/shard_map/pallas_call | solution.py:449
  146.0 1.7 %copy.17 = bf16[128,1280]{1,0:T(8,128)(2,1)} copy(bf16[128,1280]{1,0:T(8,128)(2,1)} %shard_map.145) | data formatting | bytes 655360
